TPU v7x, 32 devices: a whole 2x2x4 slice. The times are simulated.
32 devices in a mesh: grp: 4 (over z), dev: 8 (over y, x, core).
Axes of the slice: x: 2, y: 2, z: 4, core: 2. Of those that a mesh axis runs over, the one named last changes fastest.
Arguments:
- amounts: float32 [64, 524288], P('dev', 'grp'), may hold values from -0.06 to 0.06, as said below
Outputs:
- offsets: float32 [64, 524288], P(None, ('grp', 'dev'))
Inputs may be any that keep to these rules, and one draw needn't show every extreme that they name: `amounts`: each entry lies within 0.06 of zero.
All inputs are finite; a program needn't handle non-finite values.
Results may differ from a plain program's by a relative error of at most 0.00095.
Values sent between devices are 32-bit elements; how exact they have to be, the bound alone decides.
A program may use at most 64 MiB of HBM per device.

v0:
```python
import jax
import jax.numpy as jnp
from jax import lax
from jax.sharding import PartitionSpec as P


def carried_in(value, axis, join, neutral):
    count, mine = (lax.axis_size(axis), lax.axis_index(axis))
    pieces = lax.all_gather(value, axis)
    total = jnp.full_like(value, 0) + jnp.asarray(neutral, value.dtype)

    def lap(position, total):
        longer = join(total, pieces[position])
        return jnp.where(position < mine, longer, total)

    return lax.fori_loop(0, count - 1, lap, total)


def local_scan(values):
    chans, length = values.shape
    block_len = 512
    count = length // block_len
    row_index = lax.broadcasted_iota(jnp.int32, (block_len, block_len), 0)
    col_index = lax.broadcasted_iota(jnp.int32, (block_len, block_len), 1)
    upper_ones = (row_index < col_index).astype(jnp.float32)
    blocks = values.reshape(chans * count, block_len)
    within = jnp.dot(
        blocks, upper_ones, precision=lax.Precision.HIGHEST, preferred_element_type=jnp.float32
    )
    within = within.reshape(chans, count, block_len)
    sums = jnp.sum(values.reshape(chans, count, block_len), axis=2)
    starts = jnp.cumsum(sums, axis=1) - sums
    result = (within + starts[:, :, None]).reshape(chans, length)
    return (result, jnp.sum(sums, axis=1))


def combine(earlier, later):
    return earlier + later


def relayout(values):
    return lax.all_to_all(values, "dev", split_axis=1, concat_axis=0, tiled=True)


def chain_groups(column_sum):
    return carried_in(column_sum, "grp", combine, jnp.zeros_like(column_sum))


def local(amounts):
    partial_sums, column_sum = local_scan(amounts)
    result = relayout(partial_sums + chain_groups(column_sum)[:, None])
    return result


def solution(mesh):
    return jax.shard_map(
        local,
        mesh=mesh,
        in_specs=(P("dev", "grp"),),
        out_specs=P(None, ("grp", "dev")),
        check_vma=False,
    )
```

profile of v0, /device:TPU:0, one launch (start us, length us, event | category | flops | bytes accessed | tf_op | source)
XLA Modules:
  0.0 113.7 jit_solution(17269614239907794902)
XLA Ops:
  0.0 4.9 %reshape.45 = f32[2048,512]{1,0:T(8,128)} reshape(f32[8,131072]{1,0:T(8,128)} %param.3) | data formatting | bytes 8388608 | tf_op jit(solution)/shard_map/reshape | solution.py:26
  4.9 8.2 %convolution_bitcast_fusion = f32[2048,512]{0,1:T(8,128)} fusion(f32[2048,512]{1,0:T(8,128)} %reshape.45), kind=kOutput, calls=%fused_computation.3 | convolution fusion | flops 6442975232 | bytes 8388608 | tf_op jit(solution)/shard_map/dot_general | solution.py:27
  13.1 5.3 %copy.14 = f32[2048,512]{1,0:T(8,128)} copy(f32[2048,512]{0,1:T(8,128)} %convolution_bitcast_fusion) | data formatting | bytes 8388608 | tf_op jit(solution)/shard_map/dot_general | solution.py:27
  18.5 4.9 %reshape.46 = f32[8,8,16384]{2,1,0:T(8,128)} reshape(f32[2048,512]{1,0:T(8,128)} %copy.14) | data formatting | bytes 8388608 | tf_op jit(solution)/shard_map/reshape | solution.py:30
  23.4 3.4 %reduce_sum.19 = f32[8]{0:T(128)S(1)} reduce(f32[8,131072]{1,0:T(8,128)} %param.3, f32[]{:T(128)} %constant.32.clone.1), dimensions={1}, to_apply=%region_3.4 | reduce | flops 1048568 | bytes 4194340 | tf_op jit(solution)/shard_map/reduce_sum | solution.py:34
  26.8 2.5 %reduce_sum.18 = f32[8,256]{0,1:T(8,128)S(1)} reduce(f32[8,256,512]{2,0,1:T(8,128)} %bitcast.15, f32[]{:T(128)} %constant.32.clone.1), dimensions={2}, to_apply=%region_0.0 | reduce | flops 1046528 | bytes 4202500 | tf_op jit(solution)/shard_map/reduce_sum | solution.py:31
  29.3 0.1 copy.16
  29.4 0.1 copy.15
  29.5 0.6 reduce-window.6
  30.0 0.2 slice_reduce_fusion
  30.2 0.1 bitcast_subtract_fusion
  30.3 2.4 %add.49 = f32[8,256,512]{2,1,0:T(8,128)} broadcast(f32[8,256]{1,0:T(8,128)S(1)} %bitcast_subtract_fusion), dimensions={0,1} | broadcast | bytes 4202496 | tf_op jit(solution)/shard_map/add | solution.py:33
  32.7 0.0 copy-start
  32.7 5.0 %add.50 = f32[8,8,16384]{2,1,0:T(8,128)} reshape(f32[8,256,512]{2,1,0:T(8,128)} %add.49) | data formatting | bytes 8388608 | tf_op jit(solution)/shard_map/add | solution.py:33
  37.7 0.0 copy-done
  37.7 0.6 dynamic-slice
  38.9 0.2 dynamic-update-slice
  39.1 13.5 %all-reduce = f32[32]{0:T(128)S(1)} all-reduce(f32[32]{0:T(128)S(1)} %dynamic-update-slice), channel_id=2, replica_groups=mesh['grp'=4,'dev'=8] {'grp'}, use_global_device_ids=true, to_apply=%add | all-reduce | flops 32 | bytes 256
  52.6 0.1 reshape.50
  52.7 0.1 while.14
  52.8 3.9 %add_add_fusion = f32[8,8,16384]{2,1,0:T(8,128)S(1)} fusion(f32[8,8,16384]{2,1,0:T(8,128)} %reshape.46, f32[8,8,16384]{2,1,0:T(8,128)} %add.50, f32[8]{0:T(128)S(1)} %get-tuple-element.84), kind=kLoop, calls=%fused_computation.2 | loop fusion | flops 2097152 | bytes 12582944 | tf_op jit(solution)/shard_map/add | solution.py:51
  56.7 2.4 %copy.17 = f32[8,8,16384]{2,0,1:T(8,128)S(1)} copy(f32[8,8,16384]{2,1,0:T(8,128)S(1)} %add_add_fusion) | data formatting | bytes 8388608 | tf_op jit(solution)/shard_map/add | solution.py:51
  59.1 52.6 %all_to_all.16 = f32[8,8,16384]{2,0,1:T(8,128)S(1)} all-to-all(f32[8,8,16384]{2,0,1:T(8,128)S(1)} %copy.17), channel_id=1, replica_groups=mesh['grp'=4,'dev'=8] {'dev'}, dimensions={1} | all-to-all | bytes 8388608 | tf_op jit(solution)/shard_map/all_to_all | solution.py:42
  111.7 2.0 %copy.26 = f32[64,16384]{1,0:T(8,128)} copy(f32[64,16384]{1,0:T(8,128)S(1)} %bitcast.16) | data formatting | bytes 8388608
  (7 shorter events, 0.1 us)
Async XLA Ops:
  32.7 5.0 %copy-start = (u32[32]{0:T(128)S(1)}, u32[32]{0:T(128)}, u32[]{:S(2)}) copy-start(u32[32]{0:T(128)} %constant.37) | copy-start | bytes 388
where the time goes:
time: 114 us
  blocking collectives  66 us (58%)
  local copies, waits for them, and re-layouts  28.2 us (25%)
  other arithmetic  10.6 us (9%)
  matrix products  8.18 us (7%)
    all_to_all x1, blocking collectives, relayout(): lax.all_to_all(values, 'dev', split_axis=1, concat_axis=0, tiled=True)  52.6 us
    unnamed x1, blocking collectives  13.5 us
    dot_general x1, matrix products, local_scan(): jnp.dot(blocks, upper_ones, precision=lax.Precision.HIGHEST, preferred_el...  8.18 us
    add x2, local copies, waits for them, and re-layouts, local_scan(): result = (within + starts[:, :, None]).reshape(chans, length)  7.34 us
    dot_general x1, local copies, waits for them, and re-layouts, local_scan(): jnp.dot(blocks, upper_ones, precision=lax.Precision.HIGHEST, preferred_el...  5.34 us
    reshape x1, local copies, waits for them, and re-layouts, local_scan(): blocks = values.reshape(chans * count, block_len)  4.95 us
    reshape x1, local copies, waits for them, and re-layouts, local_scan(): within = within.reshape(chans, count, block_len)  4.94 us
    add x1, other arithmetic, local(): result = relayout(partial_sums + chain_groups(column_sum)[:, None])  3.92 us

commit v1 on v0

v1 whole, which is shorter than its diff:
```python
import functools

import jax
import jax.numpy as jnp
from jax import lax
from jax.experimental import pallas as pl
from jax.experimental.pallas import tpu as pltpu
from jax.sharding import PartitionSpec as P

MESH = pl.DeviceIdType.MESH
LANES = 128


def partner(me, k, n):
    if n & (n - 1):
        return lax.rem(me + k, n)
    other, bit = me, 1
    while bit < n:
        if k & bit:
            other = other + bit - 2 * bit * lax.rem(me // bit, 2)
        bit *= 2
    return other


def visit_order(n):
    return [*range(2, n, 2), *range(3, n, 2), *range(1, min(n, 2)), 0]


def piece_spans(rows):
    cuts = [0, rows // 8, rows // 4, rows // 2, rows]
    return list(zip(cuts[:-1], cuts[1:]))


def kernel(n, groups, x_ref, t_ref, carry_ref, x_vm, s_vm, w_vm, run_vm, group_vm, give_vm,
           load_sem, send_sem, recv_sem, csend_sem, crecv_sem, zsend_sem, zrecv_sem):
    me, grp = lax.axis_index("dev"), lax.axis_index("grp")
    chans, rows = t_ref.shape[1:]
    order = visit_order(n)
    spans = piece_spans(rows)
    others = {k: partner(me, k, n) for k in order}

    barrier = pltpu.get_barrier_semaphore()
    for k in order:
        if k:
            pl.semaphore_signal(barrier, inc=1, device_id={"dev": others[k]}, device_id_type=MESH)

    @pl.when(grp > 0)
    def _():
        pl.semaphore_signal(barrier, inc=1, device_id={"grp": grp - 1}, device_id_type=MESH)

    @pl.when(grp < groups - 1)
    def _():
        pl.semaphore_signal(barrier, inc=1, device_id={"grp": grp + 1}, device_id_type=MESH)

    def load(piece, k):
        lo, hi = spans[piece]
        at = pl.ds(pl.multiple_of(others[k] * rows + lo, LANES), hi - lo)
        return pltpu.make_async_copy(x_ref.at[:, at], x_vm.at[:, at], load_sem.at[piece, k])

    for piece in range(len(spans)):
        for k in order:
            load(piece, k).start()

    shape = (2 * LANES, 2 * LANES)
    row = lax.rem(lax.broadcasted_iota(jnp.int32, shape, 0), LANES)
    col = lax.broadcasted_iota(jnp.int32, shape, 1)
    w_vm[...] = jnp.where((row < col) | (col >= LANES), 1.0, 0.0).astype(jnp.bfloat16)
    run_vm[...] = jnp.zeros_like(run_vm)

    tile = min(rows // 8, 2048)
    steps = tile // LANES

    def scan(piece, k):
        lo, hi = spans[piece]
        base = others[k] * rows
        dest = t_ref.at[me] if k == 0 else s_vm.at[others[k]]

        def one(i, run):
            start = lo + i * tile
            block = x_vm[:, pl.ds(pl.multiple_of(base + start, LANES), tile)]
            stack = jnp.concatenate(
                [block[:, j * LANES:(j + 1) * LANES] for j in range(steps)], axis=0)
            high = stack.astype(jnp.bfloat16)
            rest = stack - high.astype(jnp.float32)
            mid = rest.astype(jnp.bfloat16)
            low = (rest - mid.astype(jnp.float32)).astype(jnp.bfloat16)
            sums = jnp.dot(jnp.concatenate([high, mid], axis=1), w_vm[...],
                           preferred_element_type=jnp.float32)
            sums = sums + jnp.dot(low, w_vm[:LANES, :], preferred_element_type=jnp.float32)
            for j in range(steps):
                part = sums[j * chans:(j + 1) * chans]
                at = pl.ds(pl.multiple_of(start + j * LANES, LANES), LANES)
                dest[:, at] = part[:, :LANES] + run
                run = run + part[:, LANES:]
            return run

        run_vm[others[k]] = lax.fori_loop(0, (hi - lo) // tile, one, run_vm[others[k]])

    def send(piece, k):
        lo, hi = spans[piece]
        at = pl.ds(lo, hi - lo)
        pltpu.make_async_remote_copy(
            src_ref=s_vm.at[others[k], :, at], dst_ref=t_ref.at[me, :, at],
            send_sem=send_sem.at[others[k]], recv_sem=recv_sem.at[me],
            device_id={"dev": others[k]}, device_id_type=MESH).start()

    near = jnp.where(grp > 0, 1, 0) + jnp.where(grp < groups - 1, 1, 0)
    late = None
    for piece in range(len(spans)):
        for k in order:
            load(piece, k).wait()
            scan(piece, k)
            if late is None and piece == 0:
                pl.semaphore_wait(barrier, n - 1 + near)
            if late is not None:
                send(*late)
            late = (piece, k) if k else None

    total = jnp.zeros((chans, LANES), jnp.float32)
    for j in range(n):
        give_vm[j] = total
        total = total + run_vm[j]

    def pass_on():
        return pltpu.make_async_remote_copy(
            src_ref=group_vm.at[1], dst_ref=group_vm.at[0], send_sem=zsend_sem, recv_sem=zrecv_sem,
            device_id={"grp": grp + 1}, device_id_type=MESH)

    @pl.when(grp == 0)
    def _():
        group_vm[0] = jnp.zeros_like(total)

    @pl.when(grp > 0)
    def _():
        pass_on().wait_recv()

    before = group_vm[0]
    group_vm[1] = before + total
    for j in range(n):
        give_vm[j] = give_vm[j] + before
    carry_ref[me] = give_vm[me]

    @pl.when(grp < groups - 1)
    def _():
        pass_on().start()

    def give(k, source):
        return pltpu.make_async_remote_copy(
            src_ref=give_vm.at[others[k]], dst_ref=carry_ref.at[source],
            send_sem=csend_sem.at[others[k]], recv_sem=crecv_sem.at[source],
            device_id={"dev": others[k]}, device_id_type=MESH)

    for k in order:
        if k:
            give(k, me).start()

    @pl.when(grp < groups - 1)
    def _():
        pass_on().wait_send()

    for k in order:
        if k:
            pltpu.make_async_remote_copy(
                src_ref=s_vm.at[others[k]], dst_ref=t_ref.at[others[k]],
                send_sem=send_sem.at[others[k]], recv_sem=recv_sem.at[others[k]],
                device_id={"dev": others[k]}, device_id_type=MESH).wait()
            give(k, others[k]).wait()


def solution(mesh):
    n, groups = mesh.shape["dev"], mesh.shape["grp"]

    def local(amounts):
        chans, length = amounts.shape
        rows = length // n
        f32 = jnp.float32
        table, carry = pl.pallas_call(
            functools.partial(kernel, n, groups),
            out_shape=[jax.ShapeDtypeStruct((n, chans, rows), f32),
                       jax.ShapeDtypeStruct((n, chans, LANES), f32)],
            in_specs=[pl.BlockSpec(memory_space=pl.ANY)],
            out_specs=[pl.BlockSpec(memory_space=pltpu.VMEM)] * 2,
            scratch_shapes=[
                pltpu.VMEM((chans, length), f32),
                pltpu.VMEM((n, chans, rows), f32),
                pltpu.VMEM((2 * LANES, 2 * LANES), jnp.bfloat16),
                pltpu.VMEM((n, chans, LANES), f32),
                pltpu.VMEM((2, chans, LANES), f32),
                pltpu.VMEM((n, chans, LANES), f32),
                pltpu.SemaphoreType.DMA((len(piece_spans(rows)), n)),
                pltpu.SemaphoreType.DMA((n,)),
                pltpu.SemaphoreType.DMA((n,)),
                pltpu.SemaphoreType.DMA((n,)),
                pltpu.SemaphoreType.DMA((n,)),
                pltpu.SemaphoreType.DMA,
                pltpu.SemaphoreType.DMA,
            ],
            compiler_params=pltpu.CompilerParams(collective_id=0, has_side_effects=True),
            name="exchange",
        )(amounts)
        return (table + carry[:, :, :1]).reshape(n * chans, rows)

    return jax.shard_map(
        local,
        mesh=mesh,
        in_specs=(P("dev", "grp"),),
        out_specs=P(None, ("grp", "dev")),
        check_vma=False,
    )
```

time: 114 us -> 59.6 us (0.52)
  blocking collectives: 66 us -> 0 us
  Pallas kernels: 0 us -> 53.9 us
  local copies, waits for them, and re-layouts: 28.2 us -> 0.84 us
  matrix products: 8.18 us -> 0 us
  other arithmetic: 10.6 us -> 4.59 us
    pallas_call x0 -> x1, Pallas kernels: none -> 53.9 us  [local(): pl.pallas_call(functools.partial(kernel, n, groups), out_shape=[jax.Shape...]
    all_to_all x1 -> x0, blocking collectives: 52.6 us -> none  [relayout(): lax.all_to_all(values, 'dev', split_axis=1, concat_axis=0, tiled=True)]
    unnamed x1 -> x0, blocking collectives: 13.5 us -> none
    reshape x3 -> x0, local copies, waits for them, and re-layouts: 9.95 us -> none  [the longest x1 4.95 us: local_scan(): blocks = values.reshape(chans * count, block_len)]
    add x3 -> x0, local copies, waits for them, and re-layouts: 9.77 us -> none  [the longest x2 7.34 us: local_scan(): result = (within + starts[:, :, None]).reshape(chans, length)]
    dot_general x1 -> x0, matrix products: 8.18 us -> none  [local_scan(): jnp.dot(blocks, upper_ones, precision=lax.Precision.HIGHEST, preferred_el...]
    reduce_sum x2 -> x0, other arithmetic: 5.92 us -> none  [the longest x1 3.38 us: local_scan(): return (result, jnp.sum(sums, axis=1))]
    dot_general x1 -> x0, local copies, waits for them, and re-layouts: 5.34 us -> none  [local_scan(): jnp.dot(blocks, upper_ones, precision=lax.Precision.HIGHEST, preferred_el...]
where the time goes in v1:
time: 59.6 us; the launch traced here: 59.4 us
  Pallas kernels  53.9 us (90%)
  other arithmetic  4.59 us (8%)
  local copies, waits for them, and re-layouts  0.84 us (1%)
    pallas_call x1, Pallas kernels, local(): pl.pallas_call(functools.partial(kernel, n, groups), out_shape=[jax.Shape...  53.9 us
    reshape x1, other arithmetic, local(): return (table + carry[:, :, :1]).reshape(n * chans, rows)  4.59 us

profile of v1, /device:TPU:0, one launch (start us, length us, event | category | flops | bytes accessed | tf_op | source)
XLA Modules:
  0.0 59.4 jit_solution(2069304783050129773)
XLA Ops:
  0.0 53.9 %exchange.1 = (f32[8,8,16384]{2,1,0:T(8,128)}, f32[8,8,128]{2,1,0:T(8,128)}) custom-call(f32[8,131072]{1,0:T(8,128)} %x_ref.1), custom_call_target="tpu_custom_call" | custom-call | tf_op jit(solution)/shard_map/exchange/pallas_call | solution.py:177
  53.9 0.8 %slice_reduce_fusion = f32[8,8]{1,0:T(8,128)S(1)} fusion(f32[8,8,128]{2,1,0:T(8,128)} %get-tuple-element.8), kind=kLoop, calls=%fused_computation.1 | loop fusion | bytes 512 | tf_op jit(solution)/shard_map/slice | solution.py:201
  54.8 4.6 %add_bitcast_fusion = f32[64,16384]{1,0:T(8,128)} fusion(f32[8,8,16384]{2,1,0:T(8,128)} %get-tuple-element.7, f32[8,8]{1,0:T(8,128)S(1)} %slice_reduce_fusion), kind=kLoop, calls=%fused_computation | loop fusion | flops 1048576 | bytes 8388864 | tf_op jit(solution)/shard_map/reshape | solution.py:201

commit v2 on v1

--- a/solution.py
+++ b/solution.py
@@ -9,6 +9,7 @@
 
 MESH = pl.DeviceIdType.MESH
 LANES = 128
+VMEM_GRANT = 46 << 20
 
 
 def partner(me, k, n):
@@ -167,6 +168,28 @@
             give(k, others[k]).wait()
 
 
+def finish(n, t_ref, carry_ref, out_ref, stage, sem):
+    rows = t_ref.shape[2]
+    step = min(rows, 16 * LANES)
+
+    def copy(j):
+        return pltpu.make_async_copy(stage.at[j], out_ref.at[j], sem.at[j])
+
+    for j in range(n):
+        carry = carry_ref[j]
+        wide = jnp.concatenate([carry] * (step // LANES), axis=1)
+
+        def add(i, _):
+            at = pl.ds(pl.multiple_of(i * step, LANES), step)
+            stage[j, :, at] = t_ref[j, :, at] + wide
+            return 0
+
+        lax.fori_loop(0, rows // step, add, 0, unroll=True)
+        copy(j).start()
+    for j in range(n):
+        copy(j).wait()
+
+
 def solution(mesh):
     n, groups = mesh.shape["dev"], mesh.shape["grp"]
 
@@ -195,10 +218,23 @@
                 pltpu.SemaphoreType.DMA,
                 pltpu.SemaphoreType.DMA,
             ],
-            compiler_params=pltpu.CompilerParams(collective_id=0, has_side_effects=True),
+            compiler_params=pltpu.CompilerParams(
+                collective_id=0, has_side_effects=True, vmem_limit_bytes=VMEM_GRANT),
             name="exchange",
         )(amounts)
-        return (table + carry[:, :, :1]).reshape(n * chans, rows)
+        out = pl.pallas_call(
+            functools.partial(finish, n),
+            out_shape=jax.ShapeDtypeStruct((n, chans, rows), f32),
+            in_specs=[pl.BlockSpec(memory_space=pltpu.VMEM)] * 2,
+            out_specs=pl.BlockSpec(memory_space=pl.ANY),
+            scratch_shapes=[
+                pltpu.VMEM((n, chans, rows), f32),
+                pltpu.SemaphoreType.DMA((n,)),
+            ],
+            compiler_params=pltpu.CompilerParams(vmem_limit_bytes=VMEM_GRANT),
+            name="finish",
+        )(table, carry)
+        return out.reshape(n * chans, rows)
 
     return jax.shard_map(
         local,

time: 59.6 us -> 54.2 us (0.909)
  other arithmetic: 4.59 us -> 0 us
  local copies, waits for them, and re-layouts: 0.84 us -> 0 us
    reshape x1 -> x0, other arithmetic: 4.59 us -> none  [local(): return (table + carry[:, :, :1]).reshape(n * chans, rows)]
    pallas_call x0 -> x1, Pallas kernels: none -> 2.11 us  [local(): pl.pallas_call(functools.partial(finish, n), out_shape=jax.ShapeDtypeStru...]
    pallas_call x1, Pallas kernels: 53.9 us -> 52 us  [local(): pl.pallas_call(functools.partial(kernel, n, groups), out_shape=[jax.Shape...]
    slice x1 -> x0, local copies, waits for them, and re-layouts: 0.84 us -> none  [local(): return (table + carry[:, :, :1]).reshape(n * chans, rows)]
where the time goes in v2:
time: 54.2 us; the launch traced here: 54.1 us
  Pallas kernels  54.1 us (100%)
    pallas_call x1, Pallas kernels, local(): pl.pallas_call(functools.partial(kernel, n, groups), out_shape=[jax.Shape...  52 us
    pallas_call x1, Pallas kernels, local(): pl.pallas_call(functools.partial(finish, n), out_shape=jax.ShapeDtypeStru...  2.11 us

profile of v2, /device:TPU:0, one launch (start us, length us, event | category | flops | bytes accessed | tf_op | source)
XLA Modules:
  0.0 54.1 jit_solution(11227460314723818589)
XLA Ops:
  0.0 52.0 %exchange.1 = (f32[8,8,16384]{2,1,0:T(8,128)S(1)}, f32[8,8,128]{2,1,0:T(8,128)S(1)}) custom-call(f32[8,131072]{1,0:T(8,128)} %x_ref.1), custom_call_target="tpu_custom_call" | custom-call | tf_op jit(solution)/shard_map/exchange/pallas_call | solution.py:200
  52.0 2.1 %finish.1 = f32[8,8,16384]{2,1,0:T(8,128)} custom-call(f32[8,8,16384]{2,1,0:T(8,128)S(1)} %get-tuple-element.7.t_ref, f32[8,8,128]{2,1,0:T(8,128)S(1)} %get-tuple-element.8.carry_ref), custom_call_target="tpu_custom_call" | custom-call | tf_op jit(solution)/shard_map/finish/pallas_call | solution.py:225

commit v3 on v2

--- a/solution.py
+++ b/solution.py
@@ -27,13 +27,22 @@
     return [*range(2, n, 2), *range(3, n, 2), *range(1, min(n, 2)), 0]
 
 
+def greeting(n):
+    if n & (n - 1) or n < 8:
+        return list(range(1, n)), []
+    across = (1 << (n.bit_length() - 2) // 2) - 1 << 1
+    down = n - 2 - across
+    near = [k for k in range(1, n) if not (k & across and k & down)]
+    return near, [k for k in near if not k & (down | 1)]
+
+
 def piece_spans(rows):
-    cuts = [0, rows // 8, rows // 4, rows // 2, rows]
+    cuts = [0, rows // 8, rows // 2, rows]
     return list(zip(cuts[:-1], cuts[1:]))
 
 
 def kernel(n, groups, x_ref, t_ref, carry_ref, x_vm, s_vm, w_vm, run_vm, group_vm, give_vm,
-           load_sem, send_sem, recv_sem, csend_sem, crecv_sem, zsend_sem, zrecv_sem):
+           load_sem, send_sem, recv_sem, rsend_sem, rrecv_sem, csend_sem, crecv_sem, zsend_sem, zrecv_sem, ready_sem):
     me, grp = lax.axis_index("dev"), lax.axis_index("grp")
     chans, rows = t_ref.shape[1:]
     order = visit_order(n)
@@ -41,9 +50,9 @@
     others = {k: partner(me, k, n) for k in order}
 
     barrier = pltpu.get_barrier_semaphore()
-    for k in order:
-        if k:
-            pl.semaphore_signal(barrier, inc=1, device_id={"dev": others[k]}, device_id_type=MESH)
+    near, relays = greeting(n)
+    for k in near:
+        pl.semaphore_signal(barrier, inc=1, device_id={"dev": partner(me, k, n)}, device_id_type=MESH)
 
     @pl.when(grp > 0)
     def _():
@@ -63,22 +72,13 @@
             load(piece, k).start()
 
     shape = (2 * LANES, 2 * LANES)
-    row = lax.rem(lax.broadcasted_iota(jnp.int32, shape, 0), LANES)
-    col = lax.broadcasted_iota(jnp.int32, shape, 1)
-    w_vm[...] = jnp.where((row < col) | (col >= LANES), 1.0, 0.0).astype(jnp.bfloat16)
-    run_vm[...] = jnp.zeros_like(run_vm)
-
     tile = min(rows // 8, 2048)
     steps = tile // LANES
 
-    def scan(piece, k):
-        lo, hi = spans[piece]
-        base = others[k] * rows
-        dest = t_ref.at[me] if k == 0 else s_vm.at[others[k]]
-
+    def scan(source, base, lo, hi, dest, run):
         def one(i, run):
             start = lo + i * tile
-            block = x_vm[:, pl.ds(pl.multiple_of(base + start, LANES), tile)]
+            block = source[:, pl.ds(pl.multiple_of(base + start, LANES), tile)]
             stack = jnp.concatenate(
                 [block[:, j * LANES:(j + 1) * LANES] for j in range(steps)], axis=0)
             high = stack.astype(jnp.bfloat16)
@@ -95,7 +95,14 @@
                 run = run + part[:, LANES:]
             return run
 
-        run_vm[others[k]] = lax.fori_loop(0, (hi - lo) // tile, one, run_vm[others[k]])
+        return lax.fori_loop(0, (hi - lo) // tile, one, run)
+
+    def raw(k, source):
+        at = pl.ds(pl.multiple_of(others[k] * rows, LANES), spans[0][1])
+        return pltpu.make_async_remote_copy(
+            src_ref=x_vm.at[:, at], dst_ref=t_ref.at[source, :, pl.ds(0, spans[0][1])],
+            send_sem=rsend_sem.at[others[k]], recv_sem=rrecv_sem.at[source],
+            device_id={"dev": others[k]}, device_id_type=MESH)
 
     def send(piece, k):
         lo, hi = spans[piece]
@@ -105,17 +112,34 @@
             send_sem=send_sem.at[others[k]], recv_sem=recv_sem.at[me],
             device_id={"dev": others[k]}, device_id_type=MESH).start()
 
-    near = jnp.where(grp > 0, 1, 0) + jnp.where(grp < groups - 1, 1, 0)
+    chained = jnp.where(grp > 0, 1, 0) + jnp.where(grp < groups - 1, 1, 0)
+    pl.semaphore_wait(barrier, len(near) + chained)
+    for k in relays:
+        pl.semaphore_signal(ready_sem, inc=1, device_id={"dev": partner(me, k, n)}, device_id_type=MESH)
+    met = False
+    for k in [*(k for k in order if k in near), *(k for k in order if k not in near)]:
+        if relays and not met and k not in near:
+            pl.semaphore_wait(ready_sem, len(relays))
+            met = True
+        load(0, k).wait()
+        if k:
+            raw(k, me).start()
+
+    row = lax.rem(lax.broadcasted_iota(jnp.int32, shape, 0), LANES)
+    col = lax.broadcasted_iota(jnp.int32, shape, 1)
+    w_vm[...] = jnp.where((row < col) | (col >= LANES), 1.0, 0.0).astype(jnp.bfloat16)
+    run_vm[...] = jnp.zeros_like(run_vm)
+
     late = None
     for piece in range(len(spans)):
         for k in order:
-            load(piece, k).wait()
-            scan(piece, k)
-            if late is None and piece == 0:
-                pl.semaphore_wait(barrier, n - 1 + near)
+            if piece:
+                load(piece, k).wait()
+            dest = s_vm.at[others[k]] if k else t_ref.at[me]
+            run_vm[others[k]] = scan(x_vm, others[k] * rows, *spans[piece], dest, run_vm[others[k]])
             if late is not None:
                 send(*late)
-            late = (piece, k) if k else None
+            late = (piece, k) if k and piece else None
 
     total = jnp.zeros((chans, LANES), jnp.float32)
     for j in range(n):
@@ -161,8 +185,15 @@
 
     for k in order:
         if k:
+            raw(k, others[k]).wait()
+            block = t_ref.at[others[k]]
+            scan(block, 0, *spans[0], block, jnp.zeros((chans, LANES), jnp.float32))
+
+    rest = pl.ds(spans[0][1], rows - spans[0][1])
+    for k in order:
+        if k:
             pltpu.make_async_remote_copy(
-                src_ref=s_vm.at[others[k]], dst_ref=t_ref.at[others[k]],
+                src_ref=s_vm.at[others[k], :, rest], dst_ref=t_ref.at[others[k], :, rest],
                 send_sem=send_sem.at[others[k]], recv_sem=recv_sem.at[others[k]],
                 device_id={"dev": others[k]}, device_id_type=MESH).wait()
             give(k, others[k]).wait()
@@ -215,8 +246,11 @@
                 pltpu.SemaphoreType.DMA((n,)),
                 pltpu.SemaphoreType.DMA((n,)),
                 pltpu.SemaphoreType.DMA((n,)),
+                pltpu.SemaphoreType.DMA((n,)),
+                pltpu.SemaphoreType.DMA((n,)),
                 pltpu.SemaphoreType.DMA,
                 pltpu.SemaphoreType.DMA,
+                pltpu.SemaphoreType.REGULAR,
             ],
             compiler_params=pltpu.CompilerParams(
                 collective_id=0, has_side_effects=True, vmem_limit_bytes=VMEM_GRANT),

time: 54.2 us -> 54.2 us (level)
  no operation moved by 1% of the time
where the time goes in v3:
time: 54.2 us; the launch traced here: 54.1 us
  Pallas kernels  54 us (100%)
    pallas_call x1, Pallas kernels, local(): pl.pallas_call(functools.partial(kernel, n, groups), out_shape=[jax.Shape...  51.9 us
    pallas_call x1, Pallas kernels, local(): pl.pallas_call(functools.partial(finish, n), out_shape=jax.ShapeDtypeStru...  2.11 us

profile of v3, /device:TPU:0, one launch (start us, length us, event | category | flops | bytes accessed | tf_op | source)
XLA Modules:
  0.0 54.1 jit_solution(12306894303513050060)
XLA Ops:
  0.0 51.9 %exchange.1 = (f32[8,8,16384]{2,1,0:T(8,128)S(1)}, f32[8,8,128]{2,1,0:T(8,128)S(1)}) custom-call(f32[8,131072]{1,0:T(8,128)} %x_ref.1), custom_call_target="tpu_custom_call" | custom-call | tf_op jit(solution)/shard_map/exchange/pallas_call | solution.py:231
  51.9 2.1 %finish.1 = f32[8,8,16384]{2,1,0:T(8,128)} custom-call(f32[8,8,16384]{2,1,0:T(8,128)S(1)} %get-tuple-element.7.t_ref, f32[8,8,128]{2,1,0:T(8,128)S(1)} %get-tuple-element.8.carry_ref), custom_call_target="tpu_custom_call" | custom-call | tf_op jit(solution)/shard_map/finish/pallas_call | solution.py:259
